TPU v7x, 32 devices: a 4x4x1 block of a 4x4x8 slice. The times are simulated.
32 devices in a mesh: dp: 1 (over z), ep: 32 (over y, x, core).
Axes of the slice: x: 4, y: 4, z: 1, core: 2. Of those that a mesh axis runs over, the one named last changes fastest.
The devices are a block of a 4x4x8 slice.
Arguments:
- resid_in: bfloat16 [4096, 2048], P(('dp', 'ep'))
- expert_ids: int32 [4096, 6], P(('dp', 'ep'))
- priority: int32 [4096, 6], P(('dp', 'ep'))
- norm_gain: float32 [2048], replicated
- router_w: bfloat16 [2048, 64], replicated
- shared_w1: bfloat16 [2048, 2816], replicated
- shared_w3: bfloat16 [2048, 2816], replicated
- shared_w2: bfloat16 [2816, 2048], replicated
- expert_w1: bfloat16 [64, 2048, 1408], P('ep')
- expert_w3: bfloat16 [64, 2048, 1408], P('ep')
- expert_w2: bfloat16 [64, 1408, 2048], P('ep')
Outputs:
- output: bfloat16 [4096, 2048], P(('dp', 'ep'))
All inputs are finite; a program needn't handle non-finite values.
Results may differ from a plain program's by a relative error of at most 0.00677691.
Values are sent between devices in bfloat16 or wider.
A program may use at most 768 MiB of HBM per device.

v0:
```python
import jax
import jax.numpy as jnp
from jax import lax
from jax.sharding import PartitionSpec as P

NORM_EPS = 1e-6
ROUTE_SCALE = 16.0


def rms_norm(resid_in, norm_gain):
    resid32 = resid_in.astype(jnp.float32)
    inv_rms = lax.rsqrt(jnp.mean(resid32 * resid32, axis=1, keepdims=True) + NORM_EPS)
    return (resid32 * inv_rms * norm_gain).astype(jnp.bfloat16)


def gate_values(normed, router_w, expert_ids):
    gate_probs = jax.nn.softmax(jnp.dot(normed, router_w, preferred_element_type=jnp.float32), axis=1)
    return ROUTE_SCALE * jnp.take_along_axis(gate_probs, expert_ids, axis=1)


def swiglu_ffn(normed, w_gate, w_up, w_down):
    up_a = jnp.dot(normed, w_gate, preferred_element_type=jnp.float32)
    up_b = jnp.dot(normed, w_up, preferred_element_type=jnp.float32)
    hidden_act = (jax.nn.silu(up_a) * up_b).astype(jnp.bfloat16)
    return jnp.dot(hidden_act, w_down, preferred_element_type=jnp.float32).astype(jnp.bfloat16)


def grouped_ffn(row_inputs, group_sizes, slot_valid, expert_w1, expert_w3, expert_w2):
    up_a = lax.ragged_dot(row_inputs, expert_w1, group_sizes, preferred_element_type=jnp.float32)
    up_b = lax.ragged_dot(row_inputs, expert_w3, group_sizes, preferred_element_type=jnp.float32)
    hidden_act = (jax.nn.silu(up_a) * up_b).astype(jnp.bfloat16)
    expert_out = lax.ragged_dot(hidden_act, expert_w2, group_sizes, preferred_element_type=jnp.float32).astype(jnp.bfloat16)
    return jnp.where(slot_valid[:, None], expert_out.astype(jnp.float32), 0.0)


def local_keep(flat_ids, prio_flat, local_experts, capacity, my_index):
    n_assign = flat_ids.shape[0]
    mine_int = (flat_ids // local_experts == my_index).astype(jnp.int32)
    by_rank = jnp.zeros((n_assign,), jnp.int32).at[prio_flat].set(mine_int)
    before = jnp.cumsum(by_rank) - by_rank
    return (mine_int > 0) & (before[prio_flat] < capacity)


def slot_layout(flat_ids, mine_kept, local_experts, capacity, my_index):
    n_assign = flat_ids.shape[0]
    local_e = flat_ids - my_index * local_experts
    sort_key = jnp.where(mine_kept, local_e, local_experts) * n_assign + jnp.arange(n_assign, dtype=jnp.int32)
    slot_order = jnp.argsort(sort_key)[:capacity]
    group_sizes = jax.ops.segment_sum(mine_kept.astype(jnp.int32), jnp.where(mine_kept, local_e, 0), num_segments=local_experts)
    return slot_order, group_sizes, mine_kept[slot_order]


def solution(mesh):
    ep_size = mesh.shape['ep']
    tok_spec = P(('dp', 'ep'))
    expert_spec = P('ep')

    def device_fn(resid_in, expert_ids, priority, norm_gain, router_w, shared_w1, shared_w3, shared_w2, expert_w1, expert_w3, expert_w2):
        tok_local = resid_in.shape[0]
        top_k = expert_ids.shape[1]
        local_experts = expert_w1.shape[0]
        capacity = tok_local * top_k
        my_index = lax.axis_index('ep')
        normed = rms_norm(resid_in, norm_gain)
        gate_vals = gate_values(normed, router_w, expert_ids)
        shared_out = swiglu_ffn(normed, shared_w1, shared_w3, shared_w2)
        all_ids = lax.all_gather(expert_ids, 'ep', tiled=True).reshape(-1)
        all_prio = lax.all_gather(priority, 'ep', tiled=True).reshape(-1)
        all_gates = lax.all_gather(gate_vals, 'ep', tiled=True).reshape(-1)
        all_normed = lax.all_gather(normed, 'ep', tiled=True)
        mine_kept = local_keep(all_ids, all_prio, local_experts, capacity, my_index)
        slot_order, group_sizes, slot_valid = slot_layout(all_ids, mine_kept, local_experts, capacity, my_index)
        tok_of = slot_order // top_k
        expert_out = grouped_ffn(all_normed[tok_of], group_sizes, slot_valid, expert_w1, expert_w3, expert_w2)
        weighted = expert_out * all_gates[slot_order][:, None]
        token_sums = jax.ops.segment_sum(weighted, tok_of, num_segments=tok_local * ep_size)
        routed = lax.psum_scatter(token_sums, 'ep', scatter_dimension=0, tiled=True)
        out_sum = resid_in.astype(jnp.float32) + shared_out.astype(jnp.float32) + routed
        return out_sum.astype(jnp.bfloat16)

    return jax.shard_map(device_fn, mesh=mesh, in_specs=(tok_spec, tok_spec, tok_spec, P(), P(), P(), P(), P(), expert_spec, expert_spec, expert_spec), out_specs=tok_spec, check_vma=False)
```

profile of v0, /device:TPU:97, one launch (start us, length us, event | category | flops | bytes accessed | tf_op | source)
XLA Modules:
  0.0 820.1 jit_solution(14692597924947013289)
XLA Ops:
  7.8 2.0 fusion.11
  10.0 32.6 %all_gather.12 = s32[4096,6]{0,1:T(8,128)S(1)} all-gather(s32[128,6]{0,1:T(8,128)} %param.12), channel_id=1, replica_groups=mesh['dp'=1,'ep'=32] {'ep'}, dimensions={0}, use_global_device_ids=true | all-gather | bytes 101376 | tf_op jit(solution)/shard_map/all_gather | solution.py:67
  43.2 1.6 reshape.188
  44.8 1.8 reshape.194
  46.6 34.2 %all_gather.13 = s32[4096,6]{0,1:T(8,128)S(1)} all-gather(s32[128,6]{0,1:T(8,128)S(1)} %copy-done.5), channel_id=1, replica_groups=mesh['dp'=1,'ep'=32] {'ep'}, dimensions={0}, use_global_device_ids=true | all-gather | bytes 101376 | tf_op jit(solution)/shard_map/all_gather | solution.py:68
  81.5 1.8 reshape.189
  83.4 90.3 %scatter_custom_fusion = s32[24576]{0:T(1024)S(1)} fusion(s32[24576]{0:T(1024)S(1)} %bitcast.20, s32[24576]{0:T(1024)S(1)} %fusion.15, s32[]{:T(128)} %constant.39.clone.1), kind=kCustom, calls=%fused_computation.48 | custom fusion | bytes 98308 | tf_op jit(solution)/shard_map/scatter | solution.py:39
  174.9 135.5 %gather_fusion = s32[24576]{0:T(1024)S(1)} fusion(s32[24576]{0:T(1024)S(1)} %bitcast_subtract_fusion, s32[24576]{0:T(1024)S(1)} %broadcast_clamp_fusion), kind=kCustom, calls=%fused_computation | custom fusion | bytes 294912 | tf_op jit(solution)/shard_map/gather | solution.py:41
  311.2 170.4 %scatter_custom_fusion.1 = s32[2]{0:T(128)} fusion(s32[24576]{0:T(1024)S(1)} %bitcast.22, s32[24576]{0:T(1024)S(1)} %get-tuple-element.21, s32[]{:T(128)} %constant.39.clone.1), kind=kCustom, calls=%fused_computation.69 | custom fusion | flops 24576 | bytes 12 | tf_op jit(solution)/shard_map/scatter-add | solution.py:49
  481.5 1.7 ragged-dot-metadata
  483.3 11.3 %sort.17 = (s32[24576]{0:T(1024)}, s32[24576]{0:T(1024)S(1)}) sort(s32[24576]{0:T(1024)S(1)} %iota_add_fusion, s32[24576]{0:T(1024)S(1)} %iota.8), dimensions={0}, to_apply=%region_5.6 | sort | flops 368640 | bytes 393216 | tf_op jit(solution)/shard_map/jit(argsort)/sort | solution.py:48
  494.6 5.0 gather_fusion.1
  500.4 5.1 gather_fusion.4
  505.7 32.4 %all_gather.15 = f32[4096,6]{0,1:T(8,128)S(1)} all-gather(f32[128,6]{0,1:T(8,128)S(1)} %select_multiply_fusion), channel_id=1, replica_groups=mesh['dp'=1,'ep'=32] {'ep'}, dimensions={0}, use_global_device_ids=true | all-gather | bytes 101376 | tf_op jit(solution)/shard_map/all_gather | solution.py:69
  540.4 4.5 gather_fusion.3
  544.9 15.0 %gather_fusion.2 = bf16[768,2048]{1,0:T(8,128)(2,1)} fusion(bf16[4096,2048]{1,0:T(8,128)(2,1)} %all-gather.2.cloned.1.call-done, s32[1024]{0:T(1024)S(1)} %pad_clamp_fusion), kind=kCustom, calls=%fused_computation.2 | custom fusion | bytes 6294528 | tf_op jit(solution)/shard_map/gather | solution.py:74
  559.9 14.8 %ragged-dot-none.2 = f32[768,1408]{1,0:T(8,128)} custom-call(s32[1]{0:T(128)} %get-tuple-element.7, s32[3]{0:T(128)} %get-tuple-element.8, s32[4]{0:T(128)} %get-tuple-element.9, s32[4]{0:T(128)} %get-tuple-element.10, s32[1]{0:T(128)} %get-tuple-element.7, bf16[768,2048]{1,0:T(8,128)(2,1)} %gather_fusion.2, bf16[2,2048,1408]{2,1,0:T(8,128)(2,1)} %param.19), custom_call_target="tpu_custom_call" | custom-call | flops 4429185024 | bytes 19005448 | tf_op jit(solution)/shard_map/ragged_dot_general/ragged-dot-none
  574.7 15.0 %ragged-dot-none.1 = f32[768,1408]{1,0:T(8,128)} custom-call(s32[1]{0:T(128)} %get-tuple-element.7, s32[3]{0:T(128)} %get-tuple-element.8, s32[4]{0:T(128)} %get-tuple-element.9, s32[4]{0:T(128)} %get-tuple-element.10, s32[1]{0:T(128)} %get-tuple-element.7, bf16[768,2048]{1,0:T(8,128)(2,1)} %gather_fusion.2, bf16[2,2048,1408]{2,1,0:T(8,128)(2,1)} %param.20), custom_call_target="tpu_custom_call" | custom-call | flops 4429185024 | bytes 19005448 | tf_op jit(solution)/shard_map/ragged_dot_general/ragged-dot-none
  589.7 6.2 multiply_convert_fusion
  595.8 15.1 %ragged-dot-none = f32[768,2048]{1,0:T(8,128)} custom-call(s32[1]{0:T(128)} %get-tuple-element.7, s32[3]{0:T(128)} %get-tuple-element.8, s32[4]{0:T(128)} %get-tuple-element.9, s32[4]{0:T(128)} %get-tuple-element.10, s32[1]{0:T(128)} %get-tuple-element.7, bf16[768,1408]{1,0:T(8,128)(2,1)} %multiply_convert_fusion, bf16[2,1408,2048]{2,1,0:T(8,128)(2,1)} %param.21), custom_call_target="tpu_custom_call" | custom-call | flops 4429185024 | bytes 19988488 | tf_op jit(solution)/shard_map/ragged_dot_general/ragged-dot-none
  610.9 29.1 %scatter_custom_fusion.2 = f32[4096,2048]{1,0:T(8,128)} fusion(s32[768]{0:T(1024)S(1)} %get-tuple-element.20, f32[]{:T(128)} %constant.24.clone.1, f32[768]{0:T(1024)S(1)} %gather_fusion.3, f32[768,2048]{1,0:T(8,128)} %ragged-dot-none, pred[768]{0:T(1024)(128)(4,1)S(1)} %gather_fusion.1), kind=kCustom, calls=%fused_computation.8 | custom fusion | flops 7864320 | bytes 39851012 | tf_op jit(solution)/shard_map/scatter-add | solution.py:76
  640.1 6.0 fusion.28
  646.1 154.5 %reduce-scatter.2.cloned.1.call-done = f32[128,2048]{1,0:T(8,128)} async-done(((f32[4096,2048]{1,0:T(8,128)}), f32[128,2048]{1,0:T(8,128)}) %reduce-scatter.2.cloned.1.call-update) | async-done | bytes 1048592 | tf_op jit(solution)/shard_map/reduce_scatter | solution.py:77
  800.6 12.2 %fusion.8 = bf16[128,2048]{1,0:T(8,128)(2,1)} fusion(f32[128,2048]{1,0:T(8,128)} %reduce-scatter.2.cloned.1.call-done, bf16[2816,2048]{1,0:T(8,128)(2,1)} %param.18, bf16[128,2048]{1,0:T(8,128)(2,1)S(1)} %copy-done.2, bf16[2048,2816]{1,0:T(8,128)(2,1)} %param.17, f32[128,2816]{1,0:T(8,128)S(1)} %fusion.28, f32[2048]{0:T(1024)S(1)} %copy-done.3, ...), kind=kOutput, calls=%fused_computation.20 | convolution fusion | flops 2957574144 | bytes 26616320 | tf_op jit(solution)/shard_map/dot_general | solution.py:25
  (55 shorter events, 8.0 us)
Async XLA Ops:
  6.5 493.3 %copy-start = (bf16[2048,64]{0,1:T(8,128)(2,1)S(1)}, bf16[2048,64]{0,1:T(8,128)(2,1)}, u32[]{:S(2)}) copy-start(bf16[2048,64]{0,1:T(8,128)(2,1)} %param.15) | copy-start | bytes 786436
  6.6 40.0 %copy-start.5 = (s32[128,6]{0,1:T(8,128)S(1)}, s32[128,6]{0,1:T(8,128)}, u32[]{:S(2)}) copy-start(s32[128,6]{0,1:T(8,128)} %param.13) | copy-start | bytes 9220
  6.6 538.3 %all-gather.2.cloned.1.call-start = ((), (), s32[]{:S(2)}) async-start(), calls=%async_computation.1 | async-start | bytes 17301504 | tf_op jit(solution)/shard_map/all_gather | solution.py:70
  9.9 790.7 %reduce-scatter.2.cloned.1.call-start = ((), (), s32[]{:S(2)}) async-start(), calls=%async_computation.2 | async-start | bytes 34603008 | tf_op jit(solution)/shard_map/reduce_scatter | solution.py:77
  174.9 324.8 %copy-start.4 = (s32[128,6]{0,1:T(8,128)S(1)}, s32[128,6]{0,1:T(8,128)}, u32[]{:S(2)}) copy-start(s32[128,6]{0,1:T(8,128)} %param.12) | copy-start | bytes 9220
  174.9 325.0 %copy-start.2 = (bf16[128,2048]{1,0:T(8,128)(2,1)S(1)}, bf16[128,2048]{1,0:T(8,128)(2,1)}, u32[]{:S(2)}) copy-start(bf16[128,2048]{1,0:T(8,128)(2,1)} %param.11) | copy-start | bytes 1572868
  174.9 325.0 %copy-start.3 = (f32[2048]{0:T(1024)S(1)}, f32[2048]{0:T(1024)}, u32[]{:S(2)}) copy-start(f32[2048]{0:T(1024)} %param.14) | copy-start | bytes 24580
  800.6 12.2 %copy-start.1 = (bf16[2048,64]{0,1:T(8,128)(2,1)S(1)}, bf16[2048,64]{0,1:T(8,128)(2,1)}, u32[]{:S(2)}) copy-start(bf16[2048,64]{0,1:T(8,128)(2,1)} %param.15) | copy-start | bytes 786436
Sparse Core Ops, SparseCore 0:
  10.1 72.7 all-gather.1
  640.2 160.3 reduce-scatter.1
where the time goes:
time: 826 us; the launch traced here: 820 us
  local copies, waits for them, and re-layouts  265 us (32%)
  other arithmetic  222 us (27%)
  waiting for transfers between devices  155 us (19%)
  blocking collectives  99.2 us (12%)
  Pallas kernels  46.6 us (6%)
  matrix products  18.5 us (2%)
  between operations  14.2 us (2%)
    scatter-add x1, other arithmetic, slot_layout(): jax.ops.segment_sum(mine_kept.astype(jnp.int32), jnp.where(mine_kept, loc...  170 us
    reduce_scatter x1, waiting for transfers between devices, device_fn(): routed = lax.psum_scatter(token_sums, 'ep', scatter_dimension=0, tiled=True)  155 us
    gather x1, local copies, waits for them, and re-layouts, local_keep(): return (mine_int > 0) & (before[prio_flat] < capacity)  136 us
    scatter x1, local copies, waits for them, and re-layouts, local_keep(): by_rank = jnp.zeros((n_assign,), jnp.int32).at[prio_flat].set(mine_int)  90.3 us
    another operation x3, Pallas kernels  44.9 us
    all_gather x1, blocking collectives, device_fn(): all_prio = lax.all_gather(priority, 'ep', tiled=True).reshape(-1)  34.2 us
    all_gather x1, blocking collectives, device_fn(): all_ids = lax.all_gather(expert_ids, 'ep', tiled=True).reshape(-1)  32.6 us
    all_gather x1, blocking collectives, device_fn(): all_gates = lax.all_gather(gate_vals, 'ep', tiled=True).reshape(-1)  32.4 us
  transfers between devices with their start and end apart: 2, of which 1 were waited for; matrix products, arithmetic and copies ran while one was open for 54% of the time, Pallas kernels for 0%

commit v1 on v0

v1 whole, which is shorter than its diff:
```python
import functools
import math

import jax
import jax.numpy as jnp
from jax import lax
from jax.experimental import pallas as pl
from jax.experimental.pallas import tpu as pltpu
from jax.sharding import PartitionSpec as P

NORM_EPS = 1e-6
ROUTE_SCALE = 16.0
MESH = pl.DeviceIdType.MESH
F32 = jnp.float32
BF16 = jnp.bfloat16
FAR = 1 << 20
TILE = 128
CAP = 72
VMEM_LIMIT = 64000 * 1024


def rms_norm(resid_in, norm_gain):
    resid32 = resid_in.astype(F32)
    inv_rms = lax.rsqrt(jnp.mean(resid32 * resid32, axis=1, keepdims=True) + NORM_EPS)
    return (resid32 * inv_rms * norm_gain).astype(BF16)


def swiglu_ffn(normed, w_gate, w_up, w_down):
    up_a = jnp.dot(normed, w_gate, preferred_element_type=F32)
    up_b = jnp.dot(normed, w_up, preferred_element_type=F32)
    hidden_act = (jax.nn.silu(up_a) * up_b).astype(BF16)
    return jnp.dot(hidden_act, w_down, preferred_element_type=F32).astype(BF16)


class Place:
    def __init__(self, ep):
        self.side = math.isqrt(ep // 2)
        self.me = lax.axis_index("ep")
        self.core = lax.rem(self.me, 2)
        self.chip = self.me // 2
        self.px = lax.rem(self.chip, self.side)
        self.py = self.chip // self.side
        self.partner = self.me + 1 - 2 * self.core

    def dev(self, dx, dy, core=None):
        x = lax.rem(self.px + dx % self.side, self.side)
        y = lax.rem(self.py + dy % self.side, self.side)
        return (y * self.side + x) * 2 + (self.core if core is None else core)

    def at(self, fam, du, dv, core=None):
        return self.dev(du, dv, core) if fam == 0 else self.dev(dv, du, core)


def tri(n, m, rows_first):
    i = lax.broadcasted_iota(jnp.int32, (n, m), 0)
    j = lax.broadcasted_iota(jnp.int32, (n, m), 1)
    return jnp.where(i < j if rows_first else j < i, 1.0, 0.0).astype(BF16)


def mm(a, b):
    return jnp.dot(a.astype(BF16), b.astype(BF16), preferred_element_type=F32)


def route(pc, ep, top_k, n_local, n_chips, meta_all, ids, prs, pr, thr, cnt, kch, pos, ka, kb, info_ref, q_ref, mx_ref):
    n_exp = ep * n_local
    tok = ids.shape[2]
    capacity = tok * top_k
    n_bits = (ep * capacity).bit_length()

    def unpack(s, _):
        for k in range(top_k):
            ids[k, pl.ds(s, 1), :] = meta_all[s, k : k + 1, :]
            prs[k, pl.ds(s, 1), :] = meta_all[s, 8 + k : 9 + k, :]
        return 0

    lax.fori_loop(0, ep, unpack, 0)

    def per_expert(e, _):
        best = jnp.full((ep, tok), FAR, jnp.int32)
        for k in range(top_k):
            best = jnp.minimum(best, jnp.where(ids[k] == e, prs[k], FAR))
        pr[e] = best
        return 0

    lax.fori_loop(0, n_exp, per_expert, 0)

    thr[...] = jnp.zeros(thr.shape, jnp.int32)

    def bit_step(i, step):
        for d in range(ep):
            cand = thr[d : d + 1, :] + step
            hits = jnp.zeros((ep, tok), F32)
            for l in range(n_local):
                hits = hits + jnp.where(pr[d * n_local + l] < cand, 1.0, 0.0)
            cnt[d : d + 1, :] = jnp.sum(hits, axis=0, keepdims=True)
        total = jnp.sum(cnt[...], axis=1, keepdims=True)
        thr[...] = thr[...] + jnp.where(total <= capacity, step, 0)
        return step // 2

    lax.fori_loop(0, n_bits, bit_step, jnp.int32(1 << (n_bits - 1)))

    def chip_counts(d, _):
        kept = jnp.zeros((ep, tok), F32)
        for l in range(n_local):
            kept = kept + jnp.where(pr[d * n_local + l] < thr[pl.ds(d, 1), :], 1.0, 0.0)
        kch[pl.ds(pl.multiple_of(d * ep, ep), ep), :] = kept
        return 0

    lax.fori_loop(0, ep, chip_counts, 0)
    pairs = kch[pl.ds(0, ep * n_chips, stride=2), :] + kch[pl.ds(1, ep * n_chips, stride=2), :]
    worst = jnp.max(jnp.sum(pairs, axis=1, keepdims=True), axis=0, keepdims=True)
    mx_ref[...] = jnp.broadcast_to(worst, mx_ref.shape).astype(jnp.int32)

    upper = tri(tok, tok, True)
    ones = jnp.ones((tok, tok), BF16)
    lower = tri(ep, ep, False)
    my_thr = thr[pl.ds(pc.me, 1), :]
    base = jnp.zeros((1, tok), F32)
    for l in range(n_local):
        kept = pr[pc.me * n_local + l] < my_thr
        kept_f = jnp.where(kept, 1.0, 0.0)
        in_row = mm(kept_f, upper)
        row_total = mm(kept_f, ones)
        row_start = mm(lower, row_total)
        pos[l] = jnp.where(kept, (in_row + row_start + base), -1.0).astype(jnp.int32)
        info_ref[2 * l] = row_total.astype(jnp.int32)
        info_ref[2 * l + 1] = (row_start + base).astype(jnp.int32)
        group = jnp.sum(row_total, axis=0, keepdims=True)
        base = base + jnp.floor((group + (TILE - 1)) * (1.0 / TILE)) * TILE

    def chip_rows(e, _):
        limit = thr[pl.ds(e // n_local, 1), :]
        first = pr[e, pl.ds(pc.chip * 2, 1), :]
        second = pr[e, pl.ds(pc.chip * 2 + 1, 1), :]
        ka[pl.ds(e, 1), :] = jnp.where(first < limit, 1.0, 0.0)
        kb[pl.ds(e, 1), :] = jnp.where(second < limit, 1.0, 0.0)
        return 0

    lax.fori_loop(0, n_exp, chip_rows, 0)
    k_a, k_b = ka[...], kb[...]
    tot_a = mm(k_a, ones)
    both = tot_a + mm(k_b, ones)
    i = lax.broadcasted_iota(jnp.int32, (n_exp, n_exp), 0)
    j = lax.broadcasted_iota(jnp.int32, (n_exp, n_exp), 1)
    earlier = jnp.where((j < i) & (j // n_local == i // n_local), 1.0, 0.0)
    before = mm(earlier, both)
    q_a = jnp.where(k_a > 0, mm(k_a, upper) + before, -1.0)
    q_b = jnp.where(k_b > 0, mm(k_b, upper) + tot_a + before, -1.0)
    second_core = lax.broadcasted_iota(jnp.int32, q_ref.shape, 0) * 0 + pc.core
    q_ref[...] = jnp.where(second_core == 0, q_a, q_b).astype(jnp.int32)


def dispatch_kernel(
    ep, top_k, n_local, b_ref, meta_ref, x_ref, info_ref, q_ref, mx_ref, yall, meta_all, ids, prs, pr, thr, cnt, kch, pos, ka, kb,
    sel, own_sem, m_send, m_recv, s_send, s_recv, p_send, p_recv, o_send, o_recv,
):
    pc = Place(ep)
    side, me = pc.side, pc.me
    tok, dim = b_ref.shape
    half, quarter = tok // 2, tok // 4

    barrier = pltpu.get_barrier_semaphore()

    def greet(o, _):
        pl.semaphore_signal(barrier, inc=1, device_id={"ep": lax.rem(me + o, ep)}, device_id_type=MESH)
        return 0

    lax.fori_loop(1, ep, greet, 0)
    pl.semaphore_wait(barrier, ep - 1)

    own = pltpu.make_async_copy(b_ref, yall.at[me], own_sem)
    own.start()

    def meta_copy(o, src):
        return pltpu.make_async_remote_copy(
            src_ref=meta_ref, dst_ref=meta_all.at[src], send_sem=m_send.at[o], recv_sem=m_recv.at[o],
            device_id={"ep": lax.rem(me + o, ep)}, device_id_type=MESH,
        )

    def send_meta(o, _):
        meta_copy(o, me).start()
        return 0

    lax.fori_loop(1, ep, send_meta, 0)

    def piece(fam, g, k, sent):
        j = g - 1
        hop = {0: 1, 1: -1, 2: 1, 3: -1}[k]
        dist = {0: 0 if sent else -1, 1: 0 if sent else 1, 2: -1 if sent else 2, 3: 1 if sent else 2}[k]
        du, dv = (dist, 0) if g == 0 else (j, dist)
        start = fam * half + (quarter if k == 3 else 0)
        size = half if k < 2 else quarter
        return du % side, dv % side, start, size, hop

    def link_copy(fam, g, k, sent):
        du, dv, start, size, hop = piece(fam, g, k, sent)
        block = pc.at(fam, du, dv)
        rows = yall.at[block, pl.ds(start, size), :]
        source = b_ref.at[pl.ds(start, size), :] if sent and (du, dv) == (0, 0) else rows
        target = pc.at(fam, hop, 0) if g == 0 else pc.at(fam, 0, hop)
        n = (fam * (side + 1) + g) * 4 + k
        return pltpu.make_async_remote_copy(
            src_ref=source, dst_ref=rows, send_sem=s_send.at[n], recv_sem=s_recv.at[n], device_id={"ep": target}, device_id_type=MESH
        )

    def pass_on(fam, g, k, mine):
        du, dv, start, size, _ = piece(fam, g, k, False)
        block = pc.at(fam, du, dv, pc.core if mine else 1 - pc.core)
        rows = yall.at[block, pl.ds(start, size), :]
        n = (fam * (side + 1) + g) * 4 + k
        return pltpu.make_async_remote_copy(
            src_ref=rows, dst_ref=rows, send_sem=p_send.at[n], recv_sem=p_recv.at[n], device_id={"ep": pc.partner}, device_id_type=MESH
        )

    def own_to_partner(block):
        return pltpu.make_async_remote_copy(
            src_ref=b_ref, dst_ref=yall.at[block], send_sem=o_send, recv_sem=o_recv, device_id={"ep": pc.partner}, device_id_type=MESH
        )

    for fam in range(2):
        for k in range(2):
            link_copy(fam, 0, k, True).start()
    own_to_partner(me).start()
    for fam in range(2):
        for k in range(2):
            link_copy(fam, 1, k, True).start()

    def wait_meta(o, _):
        meta_copy(o, lax.rem(me - o + ep, ep)).wait_recv()
        return 0

    meta_all[me] = meta_ref[...]
    lax.fori_loop(1, ep, wait_meta, 0)
    route(pc, ep, top_k, n_local, ep // 2, meta_all, ids, prs, pr, thr, cnt, kch, pos, ka, kb, info_ref, q_ref, mx_ref)

    slots = x_ref.shape[0]
    n_cols = 256
    started = []

    def pick(chips):
        blocks = [pc.dev(dx, dy, core) for dx, dy in chips for core in range(2)]

        def build(i, _):
            rows = pl.ds(pl.multiple_of(i * TILE, TILE), TILE)
            slot = lax.broadcasted_iota(jnp.int32, (TILE, tok), 0) + i * TILE
            for n, block in enumerate(blocks):
                hit = slot == pos[0, pl.ds(block, 1), :]
                for l in range(1, n_local):
                    hit = hit | (slot == pos[l, pl.ds(block, 1), :])
                sel[rows, n * tok : (n + 1) * tok] = jnp.where(hit, 1.0, 0.0).astype(BF16)
            return 0

        lax.fori_loop(0, slots // TILE, build, 0)
        first = not started
        started.append(chips)

        def one(n, _):
            cols = pl.ds(pl.multiple_of(n * n_cols, n_cols), n_cols)
            source = jnp.concatenate([yall[block, :, cols] for block in blocks], axis=0)
            picked = jnp.dot(sel[...], source, preferred_element_type=F32).astype(BF16)
            x_ref[:, cols] = picked if first else x_ref[:, cols] + picked
            return 0

        lax.fori_loop(0, dim // n_cols, one, 0)

    order = [(f, 0, k) for f in range(2) for k in range(2)]
    order += [(f, 1, k) for f in range(2) for k in range(2)]
    order += [(f, 0, k) for f in range(2) for k in (2, 3)]
    order += [(f, g, k) for g in (side, 2) for f in range(2) for k in range(2)]
    order += [(f, 1, k) for f in range(2) for k in (2, 3)]
    order += [(f, 3, k) for f in range(2) for k in range(2)]
    order += [(f, g, k) for g in (side, 2, 3) for f in range(2) for k in (2, 3)]

    def chip_of(fam, g, k):
        du, dv = piece(fam, g, k, False)[:2]
        return (du, dv) if fam == 0 else (dv, du)

    parts = {}
    for fam, g, k in order:
        parts[chip_of(fam, g, k)] = parts.get(chip_of(fam, g, k), 0) + 2

    complete = [(0, 0)]
    got = set()

    def landed(fam, g, k):
        chip = chip_of(fam, g, k)
        parts[chip] -= 1
        if parts[chip] == 0:
            complete.append(chip)

    own.wait()
    own_to_partner(pc.partner).wait_recv()
    lag = 4
    for i in range(len(order) + lag):
        if i < len(order):
            fam, g, k = order[i]
            link_copy(fam, g, k, False).wait_recv()
            got.add((fam, g, k))
            if k < 2:
                link_copy(fam, g, k + 2, True).start()
                if g == 0:
                    j = side - 1 if k == 0 else 1
                    for kk in range(2):
                        link_copy(fam, 1 + j, kk, True).start()
            elif g == 0 and (fam, g, 2) in got and (fam, g, 3) in got:
                for kk in range(2):
                    link_copy(fam, 3, kk, True).start()
            pass_on(fam, g, k, True).start()
            landed(fam, g, k)
        if i >= lag:
            fam, g, k = order[i - lag]
            pass_on(fam, g, k, False).wait_recv()
            landed(fam, g, k)
        while len(complete) >= 2:
            pick([complete.pop(0), complete.pop(0)])

    def sent_meta(o, _):
        meta_copy(o, me).wait_send()
        return 0

    lax.fori_loop(1, ep, sent_meta, 0)
    own_to_partner(me).wait_send()
    for fam, g, k in order:
        link_copy(fam, g, k, True).wait_send()
        pass_on(fam, g, k, True).wait_send()


def dispatch(ep, n_local, normed, expert_ids, priority):
    tok, dim = normed.shape
    top_k = expert_ids.shape[1]
    side = math.isqrt(ep // 2)
    n_exp = ep * n_local
    slots = tok * top_k + (n_local - 1) * TILE
    pad = jnp.zeros((8 - top_k, tok), jnp.int32)
    meta = jnp.concatenate([expert_ids.T, pad, priority.T, pad], axis=0)
    n_piece = 2 * (side + 1) * 4
    vmem = pl.BlockSpec(memory_space=pltpu.VMEM)
    dma = pltpu.SemaphoreType.DMA
    return pl.pallas_call(
        functools.partial(dispatch_kernel, ep, top_k, n_local),
        out_shape=(
            jax.ShapeDtypeStruct((slots, dim), BF16),
            jax.ShapeDtypeStruct((2 * n_local, ep, tok), jnp.int32),
            jax.ShapeDtypeStruct((n_exp, tok), jnp.int32),
            jax.ShapeDtypeStruct((8, 128), jnp.int32),
        ),
        in_specs=[vmem, vmem],
        out_specs=(vmem, vmem, vmem, vmem),
        scratch_shapes=[
            pltpu.VMEM((ep, tok, dim), BF16),
            pltpu.VMEM((ep, 16, tok), jnp.int32),
            pltpu.VMEM((top_k, ep, tok), jnp.int32),
            pltpu.VMEM((top_k, ep, tok), jnp.int32),
            pltpu.VMEM((n_exp, ep, tok), jnp.int32),
            pltpu.VMEM((ep, tok), jnp.int32),
            pltpu.VMEM((ep, tok), F32),
            pltpu.VMEM((ep * ep, tok), F32),
            pltpu.VMEM((n_local, ep, tok), jnp.int32),
            pltpu.VMEM((n_exp, tok), F32),
            pltpu.VMEM((n_exp, tok), F32),
            pltpu.VMEM((slots, 4 * tok), BF16),
            dma(()), dma((ep,)), dma((ep,)), dma((n_piece,)), dma((n_piece,)), dma((n_piece,)), dma((n_piece,)), dma(()), dma(()),
        ],
        compiler_params=pltpu.CompilerParams(collective_id=0, has_side_effects=True, vmem_limit_bytes=VMEM_LIMIT),
        name="dispatch",
    )(normed, meta)


def expert_kernel(sc, x_ref, w1_hbm, w3_hbm, w2_hbm, e_ref, w1, w3, w2, sems):
    n_local, ep = w1.shape[0], sc.shape[1]
    slots = x_ref.shape[0]
    loads = []
    for l in range(n_local):
        for n, (src, dst) in enumerate(((w1_hbm, w1), (w3_hbm, w3), (w2_hbm, w2))):
            loads.append(pltpu.make_async_copy(src.at[l], dst.at[l], sems.at[l, n]))
            loads[-1].start()
    tiles = [(sc[2 * l + 1, ep - 1] - sc[2 * l + 1, 0] + sc[2 * l, ep - 1] + TILE - 1) // TILE for l in range(n_local)]
    done = 0
    for l in range(n_local):
        loads[3 * l].wait()
        loads[3 * l + 1].wait()
        loads[3 * l + 2].wait()

        def one(i, _, l=l, done=done):
            rows = pl.ds(pl.multiple_of((done + i) * TILE, TILE), TILE)
            x = x_ref[rows, :]
            up_a = jnp.dot(x, w1[l], preferred_element_type=F32)
            up_b = jnp.dot(x, w3[l], preferred_element_type=F32)
            act = (up_a * jax.nn.sigmoid(up_a) * up_b).astype(BF16)
            e_ref[rows, :] = jnp.dot(act, w2[l], preferred_element_type=F32).astype(BF16)
            return 0

        lax.fori_loop(0, tiles[l], one, 0)
        done = done + tiles[l]

    def clear(i, _):
        rows = pl.ds(pl.multiple_of(i * TILE, TILE), TILE)
        e_ref[rows, :] = jnp.zeros((TILE, e_ref.shape[1]), BF16)
        return 0

    lax.fori_loop(done, slots // TILE, clear, 0)


def experts(scalars, x, expert_w1, expert_w3, expert_w2):
    vmem = pl.BlockSpec(memory_space=pltpu.VMEM)
    hbm = pl.BlockSpec(memory_space=pl.ANY)
    n_local, dim, ff = expert_w1.shape
    return pl.pallas_call(
        expert_kernel,
        out_shape=jax.ShapeDtypeStruct(x.shape, BF16),
        in_specs=[pl.BlockSpec(memory_space=pltpu.SMEM), vmem, hbm, hbm, hbm],
        out_specs=vmem,
        scratch_shapes=[
            pltpu.VMEM((n_local, dim, ff), BF16),
            pltpu.VMEM((n_local, dim, ff), BF16),
            pltpu.VMEM((n_local, ff, dim), BF16),
            pltpu.SemaphoreType.DMA((n_local, 3)),
        ],
        compiler_params=pltpu.CompilerParams(vmem_limit_bytes=VMEM_LIMIT),
        name="experts",
    )(scalars, x, expert_w1, expert_w3, expert_w2)


def fill_kernel(ep, sc, rnd, e_ref, a_ref, b_ref):
    pc = Place(ep)
    side = pc.side
    slots, dim = e_ref.shape
    n_local = sc.shape[0] // 2
    width = dim // 4
    window = (CAP + 15 + 15) // 16 * 16
    skip = rnd[0] * CAP

    def one(n, _):
        dx, dy = lax.rem(n, side), n // side
        chip = lax.rem(pc.py + dy, side) * side + lax.rem(pc.px + dx, side)
        row = lax.broadcasted_iota(jnp.int32, (CAP, window), 0)
        col = lax.broadcasted_iota(jnp.int32, (CAP, window), 1)
        picks, sources = [], []
        lead = -skip
        for l in range(n_local):
            start, count = sc[2 * l + 1, 2 * chip], sc[2 * l, 2 * chip] + sc[2 * l, 2 * chip + 1]
            used = jnp.minimum(jnp.maximum(-lead, 0), count)
            origin = jnp.minimum((start + used) // 16 * 16, slots - window)
            origin = pl.multiple_of(origin, 16)
            slot = row - lead + start
            hit = (slot == col + origin) & (row >= lead) & (row < lead + count)
            picks.append(jnp.where(hit, 1.0, 0.0).astype(BF16))
            sources.append(e_ref[pl.ds(origin, window), :])
            lead = lead + count
        out = jnp.dot(picks[0], sources[0], preferred_element_type=F32)
        for l in range(1, n_local):
            out = out + jnp.dot(picks[l], sources[l], preferred_element_type=F32)
        out = out.astype(BF16)
        for c in range(2):
            a_ref[dx, c, dy] = out[:, c * width : (c + 1) * width]
            b_ref[dy, c, dx] = out[:, (2 + c) * width : (3 + c) * width]
        return 0

    lax.fori_loop(0, side * side, one, 0)


def fill(ep, scalars, rnd, e):
    side = math.isqrt(ep // 2)
    vmem = pl.BlockSpec(memory_space=pltpu.VMEM)
    smem = pl.BlockSpec(memory_space=pltpu.SMEM)
    bucket = jax.ShapeDtypeStruct((side, 2, side, CAP, e.shape[1] // 4), BF16)
    return pl.pallas_call(
        functools.partial(fill_kernel, ep),
        out_shape=(bucket, bucket),
        in_specs=[smem, smem, vmem],
        out_specs=(vmem, vmem),
        compiler_params=pltpu.CompilerParams(vmem_limit_bytes=VMEM_LIMIT),
        name="fill",
    )(scalars, rnd, e)


def combine_kernel(
    ep, n_local, bka, bkb, q_ref, p_ref, acc_ref, out_ref, st, rl, fin, ry, pf, g_ref, s_send, s_recv, p_send, p_recv
):
    pc = Place(ep)
    side = pc.side
    tok = q_ref.shape[1]
    width = bka.shape[-1]
    bk = (bka, bkb)

    barrier = pltpu.get_barrier_semaphore()
    friends = [pc.dev(1, 0), pc.dev(-1, 0), pc.dev(0, 1), pc.dev(0, -1), pc.partner]
    for friend in friends:
        pl.semaphore_signal(barrier, inc=1, device_id={"ep": friend}, device_id_type=MESH)
    pl.semaphore_wait(barrier, len(friends))

    def held(fam, j):
        return bk[fam].at[0] if j == 0 else st.at[fam, j]

    def link_copy(fam, g, k):
        hop = 1 if k % 2 == 0 else -1
        c = k % 2
        if g == 0:
            target = pc.at(fam, hop, 0)
            if k < 2:
                src, dst = bk[fam].at[hop % side], st.at[fam, hop % side]
            elif k < 4:
                src, dst = bk[fam].at[2, c], rl.at[fam, c]
            else:
                src, dst = rl.at[fam, c], st.at[fam, 2, c]
        else:
            j = g - 1
            target = pc.at(fam, 0, hop)
            if k < 2:
                src, dst = held(fam, j).at[:, hop % side], fin.at[fam, j, hop % side]
            elif k < 4:
                src, dst = held(fam, j).at[c, 2], ry.at[fam, j, c]
            else:
                src, dst = ry.at[fam, j, c], fin.at[fam, j, 2, c]
        n = (fam * (side + 1) + g) * 6 + k
        return pltpu.make_async_remote_copy(
            src_ref=src, dst_ref=dst, send_sem=s_send.at[n], recv_sem=s_recv.at[n], device_id={"ep": target}, device_id_type=MESH
        )

    def arrived(fam, j, v):
        return held(fam, j).at[:, 0] if v == 0 else fin.at[fam, j, v]

    def pass_on(fam, j, v):
        n = (fam * side + j) * side + v
        return pltpu.make_async_remote_copy(
            src_ref=arrived(fam, j, v), dst_ref=pf.at[fam, j, v], send_sem=p_send.at[n], recv_sem=p_recv.at[n],
            device_id={"ep": pc.partner}, device_id_type=MESH,
        )

    for k in (2, 3, 0, 1):
        for fam in range(2):
            link_copy(fam, 0, k).start()
    for k in (2, 3, 0, 1):
        for fam in range(2):
            link_copy(fam, 1, k).start()
    for fam in range(2):
        pass_on(fam, 0, 0).start()

    row = lax.broadcasted_iota(jnp.int32, (g_ref.shape[3], tok), 0)

    def weights(d, _):
        w = jnp.zeros(row.shape, F32)
        for l in range(n_local):
            e = d * n_local + l
            w = w + jnp.where(row == q_ref[pl.ds(e, 1), :], p_ref[pl.ds(e, 1), :], 0.0)
        w = w.T
        for n in range(3):
            term = w.astype(BF16)
            g_ref[d, n] = term
            w = w - term.astype(F32)
        return 0

    lax.fori_loop(0, ep, weights, 0)
    out_ref[...] = acc_ref[...]

    def add(fam, j, v):
        devs = [pc.at(fam, -j, -v), pc.at(fam, -j, -v, 1 - pc.core)]
        for c in range(2):
            cols = slice((2 * fam + c) * width, (2 * fam + c + 1) * width)
            total = out_ref[:, cols]
            for d, rows in zip(devs, (arrived(fam, j, v), pf.at[fam, j, v])):
                data = rows[c]
                for n in range(3):
                    total = total + jnp.dot(g_ref[d, n][:, :CAP], data, preferred_element_type=F32)
            out_ref[:, cols] = total

    ready = []

    def here(fam, j, v):
        pass_on(fam, j, v).start()
        ready.append((fam, j, v))

    def drain(keep):
        while len(ready) > keep:
            fam, j, v = ready.pop(0)
            pass_on(fam, j, v).wait_recv()
            add(fam, j, v)

    def got(fam, g, k):
        link_copy(fam, g, k).wait_recv()

    ready += [(0, 0, 0), (1, 0, 0)]
    for k in (2, 3):
        for fam in range(2):
            got(fam, 0, k)
            link_copy(fam, 0, k + 2).start()
    drain(0)
    for k in (0, 1):
        for fam in range(2):
            got(fam, 0, k)
            j = 1 if k == 0 else side - 1
            for kk in (2, 3, 0, 1):
                link_copy(fam, 1 + j, kk).start()
            here(fam, j, 0)
    for k in (2, 3):
        for fam in range(2):
            got(fam, 1, k)
            link_copy(fam, 1, k + 2).start()
    for fam in range(2):
        got(fam, 0, 4)
        got(fam, 0, 5)
        for kk in (2, 3, 0, 1):
            link_copy(fam, 3, kk).start()
        here(fam, 2, 0)
    drain(2)
    for j in (0, 1, side - 1, 2):
        if j > 0:
            for k in (2, 3):
                for fam in range(2):
                    got(fam, 1 + j, k)
                    link_copy(fam, 1 + j, k + 2).start()
        for k in (0, 1):
            for fam in range(2):
                got(fam, 1 + j, k)
                here(fam, j, 1 if k == 0 else side - 1)
        drain(2)
    for j in (0, 1, side - 1, 2):
        for fam in range(2):
            got(fam, 1 + j, 4)
            got(fam, 1 + j, 5)
            here(fam, j, 2)
        drain(2)
    drain(0)
    for fam in range(2):
        for g in range(side + 1):
            for k in range(6):
                link_copy(fam, g, k).wait_send()
        for j in range(side):
            for v in range(side):
                pass_on(fam, j, v).wait_send()


def combine(ep, n_local, bka, bkb, q, weights, acc):
    side = math.isqrt(ep // 2)
    cap, width = bka.shape[-2:]
    tok = q.shape[1]
    vmem = pl.BlockSpec(memory_space=pltpu.VMEM)
    dma = pltpu.SemaphoreType.DMA
    n_link, n_pass = 2 * (side + 1) * 6, 2 * side * side
    return pl.pallas_call(
        functools.partial(combine_kernel, ep, n_local),
        out_shape=jax.ShapeDtypeStruct(acc.shape, F32),
        in_specs=[vmem] * 5,
        out_specs=vmem,
        scratch_shapes=[
            pltpu.VMEM((2, side, 2, side, cap, width), BF16),
            pltpu.VMEM((2, 2, side, cap, width), BF16),
            pltpu.VMEM((2, side, side, 2, cap, width), BF16),
            pltpu.VMEM((2, side, 2, cap, width), BF16),
            pltpu.VMEM((2, side, side, 2, cap, width), BF16),
            pltpu.VMEM((ep, 3, tok, tok), BF16),
            dma((n_link,)), dma((n_link,)), dma((n_pass,)), dma((n_pass,)),
        ],
        compiler_params=pltpu.CompilerParams(collective_id=1, has_side_effects=True, vmem_limit_bytes=VMEM_LIMIT),
        name="combine",
    )(bka, bkb, q, weights, acc)


def solution(mesh):
    ep = mesh.shape["ep"]
    tok_spec = P(("dp", "ep"))
    expert_spec = P("ep")

    def device_fn(resid_in, expert_ids, priority, norm_gain, router_w, shared_w1, shared_w3, shared_w2, expert_w1, expert_w3, expert_w2):
        n_local = expert_w1.shape[0]
        normed = rms_norm(resid_in, norm_gain)
        x, info, q, worst = dispatch(ep, n_local, normed, expert_ids, priority)
        gates = ROUTE_SCALE * jax.nn.softmax(jnp.dot(normed, router_w, preferred_element_type=F32), axis=1)
        shared_out = swiglu_ffn(normed, shared_w1, shared_w3, shared_w2)
        scalars = info[:, :, 0]
        e = experts(scalars, x, expert_w1, expert_w3, expert_w2)
        rounds = (worst[0, 0] + CAP - 1) // CAP
        gates_t = gates.T

        def one_round(carry):
            rnd, acc = carry
            bka, bkb = fill(ep, scalars, rnd[None], e)
            return rnd + 1, combine(ep, n_local, bka, bkb, q - rnd * CAP, gates_t, acc)

        start = (jnp.int32(0), jnp.zeros(resid_in.shape, F32))
        routed = lax.while_loop(lambda carry: (carry[0] == 0) | (carry[0] < rounds), one_round, start)[1]
        return (resid_in.astype(F32) + shared_out.astype(F32) + routed).astype(BF16)

    return jax.shard_map(
        device_fn, mesh=mesh,
        in_specs=(tok_spec, tok_spec, tok_spec, P(), P(), P(), P(), P(), expert_spec, expert_spec, expert_spec),
        out_specs=tok_spec, check_vma=False,
    )
```

time: 826 us -> 204 us (0.25)
  local copies, waits for them, and re-layouts: 265 us -> 3.36 us
  other arithmetic: 222 us -> 5.29 us
  waiting for transfers between devices: 155 us -> 0 us
  Pallas kernels: 46.6 us -> 174 us
  blocking collectives: 99.2 us -> 0 us
  between operations: 14.2 us -> 0.78 us
    scatter-add x2 -> x0, other arithmetic: 199 us -> none  [the longest x1 170 us: slot_layout(): jax.ops.segment_sum(mine_kept.astype(jnp.int32), jnp.where(mine_kept, loc...]
    pallas_call x0 -> x4, Pallas kernels: none -> 174 us  [the longest x1 74.8 us: dispatch(): pl.pallas_call(functools.partial(dispatch_kernel, ep, top_k, n_local), ou...]
    gather x9 -> x0, local copies, waits for them, and re-layouts: 166 us -> none  [the longest x1 136 us: local_keep(): return (mine_int > 0) & (before[prio_flat] < capacity)]
    reduce_scatter x1 -> x0, waiting for transfers between devices: 155 us -> none  [device_fn(): routed = lax.psum_scatter(token_sums, 'ep', scatter_dimension=0, tiled=True)]
    all_gather x3 -> x0, blocking collectives: 99.2 us -> none  [the longest x1 34.2 us: device_fn(): all_prio = lax.all_gather(priority, 'ep', tiled=True).reshape(-1)]
    scatter x1 -> x0, local copies, waits for them, and re-layouts: 90.3 us -> none  [local_keep(): by_rank = jnp.zeros((n_assign,), jnp.int32).at[prio_flat].set(mine_int)]
    another operation x3 -> x0, Pallas kernels: 44.9 us -> none
    sort x1 -> x0, other arithmetic: 11.3 us -> none  [slot_layout(): slot_order = jnp.argsort(sort_key)[:capacity]]
  transfers between devices with their start and end apart: 2 -> 0, of which waited for: 1 -> 0; matrix products, arithmetic and copies ran while one was open for 54% -> 0% of each run, Pallas kernels for 0% -> 0%
where the time goes in v1:
time: 204 us; the launch traced here: 203 us
  Pallas kernels  174 us (85%)
  matrix products  19.6 us (10%)
  other arithmetic  5.29 us (3%)
  local copies, waits for them, and re-layouts  3.36 us (2%)
    pallas_call x1, Pallas kernels, dispatch(): pl.pallas_call(functools.partial(dispatch_kernel, ep, top_k, n_local), ou...  74.8 us
    pallas_call x1, Pallas kernels, combine(): pl.pallas_call(functools.partial(combine_kernel, ep, n_local), out_shape=...  68.8 us
    pallas_call x1, Pallas kernels, experts(): pl.pallas_call(expert_kernel, out_shape=jax.ShapeDtypeStruct(x.shape, BF1...  20.6 us
    dot_general x1, matrix products, swiglu_ffn(): return jnp.dot(hidden_act, w_down, preferred_element_type=F32).astype(BF16)  12 us
    pallas_call x1, Pallas kernels, fill(): pl.pallas_call(functools.partial(fill_kernel, ep), out_shape=(bucket, buc...  9.68 us
    dot_general x1, matrix products, swiglu_ffn(): up_a = jnp.dot(normed, w_gate, preferred_element_type=F32)  6.22 us

profile of v1, /device:TPU:97, one launch (start us, length us, event | category | flops | bytes accessed | tf_op | source)
XLA Modules:
  0.0 203.2 jit_solution(6365334067282970964)
XLA Ops:
  0.0 0.0 copy-start
  0.0 1.3 fusion.5
  1.3 2.0 fusion.7.b_ref
  3.3 1.3 pad_add_fusion.meta_ref
  4.6 74.8 %dispatch.1 = (bf16[896,2048]{1,0:T(8,128)(2,1)}, s32[4,32,128]{2,1,0:T(8,128)}, s32[64,128]{1,0:T(8,128)S(1)}, s32[8,128]{1,0:T(8,128)}) custom-call(bf16[128,2048]{1,0:T(8,128)(2,1)} %fusion.7.b_ref, s32[16,128]{1,0:T(8,128)} %pad_add_fusion.meta_ref), custom_call_target="tpu_custom_call" | custom-call | tf_op jit(solution)/shard_map/dispatch/pallas_call | solution.py:339
  79.4 1.2 slice.6
  81.3 0.0 copy-done
  81.3 1.4 fusion.16
  82.8 1.0 slice_reduce_fusion.sc
  83.8 20.6 %experts.1 = bf16[896,2048]{1,0:T(8,128)(2,1)} custom-call(s32[4,32]{1,0:T(4,128)S(1)} %slice_reduce_fusion.sc, bf16[896,2048]{1,0:T(8,128)(2,1)} %get-tuple-element.51.x_ref, bf16[2,2048,1408]{2,1,0:T(8,128)(2,1)} %w1_hbm.1, bf16[2,2048,1408]{2,1,0:T(8,128)(2,1)} %w3_hbm.1, bf16[2,1408,2048]{2,1,0:T(8,128)(2,1)} %w2_hbm.1), custom_call_target="tpu_custom_call" | custom-call | tf_op jit(solution)/shard_map/experts/pallas_call | solution.py:408
  104.3 0.1 broadcast_in_dim.6
  104.4 0.0 copy-start.3
  104.4 80.6 %while.10 = (s32[]{:T(128)}, f32[128,2048]{1,0:T(8,128)S(1)}, s32[]{:T(128)}, s32[4,32]{1,0:T(4,128)S(1)}, bf16[896,2048]{1,0:T(8,128)(2,1)}, /*index=5*/s32[64,...) while((s32[]{:T(128)}, f32[128,2048]{1,0:T(8,128)S(1)}, s32[]{:T(128)}, s32[4,32]{1,0:T(4,128)S(1)}, ...), condition=%wide.region_4.5_spmd, body=%wide.region_3.4_spmd.sunk | while | flops 8197 | bytes 2162809 | solution.py:681
  104.7 9.7 %fill.1 = (bf16[4,2,4,72,512]{4,3,2,1,0:T(8,128)(2,1)}, bf16[4,2,4,72,512]{4,3,2,1,0:T(8,128)(2,1)}) custom-call(s32[4,32]{1,0:T(4,128)S(1)} %get-tuple-element.139.sc, s32[1]{0:T(128)} %bitcast.12.rnd, bf16[896,2048]{1,0:T(8,128)(2,1)} %get-tuple-element.140.e_ref), custom_call_target="tpu_custom_call" | custom-call | tf_op jit(solution)/shard_map/while/body/fill/pallas_call | solution.py:467
  114.3 0.6 broadcast_subtract_fusion.2.q_ref
  115.0 1.1 copy.21.acc_ref
  116.0 68.8 %combine.1 = f32[128,2048]{1,0:T(8,128)S(1)} custom-call(bf16[4,2,4,72,512]{4,3,2,1,0:T(8,128)(2,1)} %get-tuple-element.116.bka, bf16[4,2,4,72,512]{4,3,2,1,0:T(8,128)(2,1)} %get-tuple-element.117.bkb, s32[64,128]{1,0:T(8,128)} %broadcast_subtract_fusion.2.q_ref, f32[64,128]{1,0:T(8,128)S(1)} %get-tuple-element.142.p_ref, f32[128,2048]{1,0:T(8,128)} %copy.21.acc_ref), custom_call_target="tpu_custom_call" | custom-call | tf_op jit(solution)/shard_map/while/body/combine/pallas_call | solution.py:640
  185.0 0.0 copy-start.2
  185.0 0.0 copy-done.3
  185.0 0.0 copy-start.1
  185.1 6.2 %fusion.14 = f32[128,2816]{1,0:T(8,128)S(1)} fusion(bf16[2048,2816]{1,0:T(8,128)(2,1)} %param.18, bf16[128,2048]{1,0:T(8,128)(2,1)} %param.13, f32[2048]{0:T(1024)S(1)} %copy-done.3, f32[128]{0:T(128)S(1)} %add_rsqrt_fusion), kind=kOutput, calls=%fused_computation.21 | convolution fusion | flops 1477443584 | bytes 13509120 | tf_op jit(solution)/shard_map/dot_general | solution.py:29
  191.3 0.0 copy-done.2
  191.3 12.0 %fusion.4 = bf16[128,2048]{1,0:T(8,128)(2,1)} fusion(f32[128,2048]{1,0:T(8,128)S(1)} %get-tuple-element.53, bf16[2816,2048]{1,0:T(8,128)(2,1)} %param.20, bf16[128,2048]{1,0:T(8,128)(2,1)S(1)} %copy-done.2, bf16[2048,2816]{1,0:T(8,128)(2,1)} %param.19, f32[128,2816]{1,0:T(8,128)S(1)} %fusion.14, f32[2048]{0:T(1024)S(1)} %copy-done.3, f32[128]{0:T(128)S(1)} %add_rsqrt_fusion), kind=kOutput, calls=%fused_computation.7 | convolution fusion | flops 2957574144 | bytes 26616320 | tf_op jit(solution)/shard_map/dot_general | solution.py:32
  203.2 0.0 copy-done.1
  (4 shorter events, 0.1 us)
Async XLA Ops:
  0.0 81.3 %copy-start = (bf16[2048,64]{0,1:T(8,128)(2,1)S(1)}, bf16[2048,64]{0,1:T(8,128)(2,1)}, u32[]{:S(2)}) copy-start(bf16[2048,64]{0,1:T(8,128)(2,1)} %param.17) | copy-start | bytes 786436
  104.4 80.6 %copy-start.3 = (f32[2048]{0:T(1024)S(1)}, f32[2048]{0:T(1024)}, u32[]{:S(2)}) copy-start(f32[2048]{0:T(1024)} %param.16) | copy-start | bytes 24580
  185.0 6.3 %copy-start.2 = (bf16[128,2048]{1,0:T(8,128)(2,1)S(1)}, bf16[128,2048]{1,0:T(8,128)(2,1)}, u32[]{:S(2)}) copy-start(bf16[128,2048]{1,0:T(8,128)(2,1)} %param.13) | copy-start | bytes 1572868
  185.0 18.2 %copy-start.1 = (bf16[2048,64]{0,1:T(8,128)(2,1)S(1)}, bf16[2048,64]{0,1:T(8,128)(2,1)}, u32[]{:S(2)}) copy-start(bf16[2048,64]{0,1:T(8,128)(2,1)} %param.17) | copy-start | bytes 786436
